TPU v7x, 32 devices: a whole 2x2x4 slice. The times are simulated.
32 devices in a mesh: row: 8 (over z, y), col: 4 (over x, core).
Axes of the slice: x: 2, y: 2, z: 4, core: 2. Of those that a mesh axis runs over, the one named last changes fastest.
Arguments:
- act_quant: bfloat16 [512, 8192], P('row', 'col'), may hold values from -127 to 127, as said below
- act_scale: float32 [512], replicated, may hold values from 0.004 to 0.04
- gate_up_quant: bfloat16 [2, 8192, 29568], P(None, 'col', 'row'), may hold values from -127 to 127, as said below
- gate_up_scale: float32 [2, 29568], P(None, 'row'), may hold values from 5e-05 to 0.0005
- down_quant: bfloat16 [29568, 8192], P('row', 'col'), may hold values from -127 to 127, as said below
- down_scale: float32 [8192], P('col'), may hold values from 3e-05 to 0.0003
Outputs:
- mixed_out: bfloat16 [512, 8192], P('row', 'col')
Inputs may be any that keep to these rules, and one draw needn't show every extreme that they name: `act_quant`: whole numbers. `gate_up_quant`: whole numbers. `down_quant`: whole numbers.
All inputs are finite; a program needn't handle non-finite values.
Results may differ from a plain program's by a relative error of at most 0.005.
Values may be sent and summed in bfloat16 or wider, within the bound.
A program may use at most 128 MiB of HBM per device.

v0:
```python
import jax
import jax.numpy as jnp
from jax import lax
from jax.sharding import PartitionSpec as P


def body(act_quant, act_scale, gate_up_quant, gate_up_scale, down_quant, down_scale):
    feature_width = gate_up_quant.shape[2]
    gathered = lax.all_gather(act_quant, "row", axis=0, tiled=True)
    share_rows = gathered.shape[0] // lax.axis_size("col")
    gate_part = jnp.dot(gathered, gate_up_quant[0], preferred_element_type=jnp.float32)
    up_part = jnp.dot(gathered, gate_up_quant[1], preferred_element_type=jnp.float32)
    summed = lax.psum_scatter(
        jnp.concatenate([gate_part, up_part], axis=1), "col", scatter_dimension=0, tiled=True
    )
    token_scale = lax.dynamic_slice_in_dim(
        act_scale, lax.axis_index("col") * share_rows, share_rows, 0
    )
    gate_val = summed[:, :feature_width] * token_scale[:, None] * gate_up_scale[0][None, :]
    up_val = summed[:, feature_width:] * token_scale[:, None] * gate_up_scale[1][None, :]
    hidden = (jax.nn.silu(gate_val) * up_val).astype(jnp.bfloat16)
    hidden = lax.all_gather(hidden, "col", axis=0, tiled=True)
    mixed_out = lax.psum_scatter(
        jnp.dot(hidden, down_quant, preferred_element_type=jnp.float32) * down_scale[None, :],
        "row",
        scatter_dimension=0,
        tiled=True,
    )
    return mixed_out.astype(jnp.bfloat16)


def solution(mesh):
    in_specs = (
        P("row", "col"),
        P(),
        P(None, "col", "row"),
        P(None, "row"),
        P("row", "col"),
        P("col"),
    )
    out_specs = P("row", "col")
    return jax.shard_map(body, mesh=mesh, in_specs=in_specs, out_specs=out_specs, check_vma=False)
```

profile of v0, /device:TPU:0, one launch (start us, length us, event | category | flops | bytes accessed | tf_op | source)
XLA Modules:
  0.0 351.1 jit_solution(16619677064941690027)
XLA Ops:
  6.5 0.0 all-gather.3.cloned.1.call-start
  6.5 0.7 all-gather.3.cloned.1.call-update
  7.3 0.0 reduce-scatter.3.cloned.1.call-start
  7.3 54.0 %all-gather.3.cloned.1.call-done = bf16[512,2048]{1,0:T(8,128)(2,1)} async-done(((bf16[64,2048]{1,0:T(8,128)(2,1)}), bf16[512,2048]{1,0:T(8,128)(2,1)}) %all-gather.3.cloned.1.call-update) | async-done | bytes 2097168 | tf_op jit(solution)/shard_map/all_gather | solution.py:9
  61.3 11.8 %fusion = f32[512,3696]{0,1:T(8,128)S(1)} fusion(bf16[512,2048]{1,0:T(8,128)(2,1)} %all-gather.3.cloned.1.call-done, bf16[2,2048,3696]{1,2,0:T(8,128)(2,1)} %param.8), kind=kOutput, calls=%fused_computation.1 | convolution fusion | flops 7751073792 | bytes 24805376 | tf_op jit(solution)/shard_map/dot_general | solution.py:12
  73.1 11.8 %fusion.2 = f32[512,3696]{0,1:T(8,128)S(1)} fusion(bf16[512,2048]{1,0:T(8,128)(2,1)} %all-gather.3.cloned.1.call-done, bf16[2,2048,3696]{1,2,0:T(8,128)(2,1)} %param.8), kind=kOutput, calls=%fused_computation.3 | convolution fusion | flops 7751073792 | bytes 24805376 | tf_op jit(solution)/shard_map/dot_general | solution.py:11
  84.9 6.2 %pad_maximum_fusion = f32[512,7392]{0,1:T(8,128)} fusion(f32[512,3696]{0,1:T(8,128)S(1)} %fusion, f32[512,3696]{0,1:T(8,128)S(1)} %fusion.2), kind=kLoop, calls=%fused_computation | loop fusion | flops 3784704 | bytes 30277632 | tf_op jit(solution)/shard_map/concatenate | solution.py:14
  91.2 0.0 copy-start
  91.2 0.0 reduce-scatter.3.cloned.1.call-update
  91.2 0.0 copy-start.1
  91.2 0.0 all-gather.5.cloned.1.call-start
  91.3 0.8 dynamic_slice.3
  92.0 0.0 copy-done
  92.0 0.1 slice_reduce_fusion.1
  92.1 110.6 %reduce-scatter.3.cloned.1.call-done = f32[128,7392]{0,1:T(8,128)} async-done(((f32[512,7392]{0,1:T(8,128)}), f32[128,7392]{0,1:T(8,128)}) %reduce-scatter.3.cloned.1.call-update) | async-done | bytes 3784720 | tf_op jit(solution)/shard_map/reduce_scatter | solution.py:13
  202.7 4.8 %fusion.8 = bf16[128,3696]{0,1:T(8,128)(2,1)} fusion(f32[128,7392]{0,1:T(8,128)} %reduce-scatter.3.cloned.1.call-done, f32[3696]{0:T(1024)S(1)} %get-tuple-element.6, f32[3696]{0:T(1024)S(1)} %get-tuple-element.5, f32[128]{0:T(128)S(1)} %dynamic_slice.3), kind=kLoop, calls=%fused_computation.11 | loop fusion | flops 4730880 | bytes 4760960 | tf_op jit(solution)/shard_map/convert_element_type | solution.py:21
  207.5 0.0 all-gather.5.cloned.1.call-update
  207.5 0.0 reduce-scatter.5.cloned.1.call-start
  207.6 32.7 %all-gather.5.cloned.1.call-done = bf16[512,3696]{0,1:T(8,128)(2,1)} async-done(((bf16[128,3696]{0,1:T(8,128)(2,1)}), bf16[512,3696]{0,1:T(8,128)(2,1)}) %all-gather.5.cloned.1.call-update) | async-done | bytes 3784720 | tf_op jit(solution)/shard_map/all_gather | solution.py:22
  240.3 0.0 copy-done.1
  240.3 14.1 %convolution_multiply_fusion = f32[512,2048]{1,0:T(8,128)} fusion(bf16[512,3696]{0,1:T(8,128)(2,1)} %all-gather.5.cloned.1.call-done, bf16[3696,2048]{1,0:T(8,128)(2,1)} %param.10, f32[2048]{0:T(1024)S(1)} %copy-done.1), kind=kOutput, calls=%fused_computation.7 | convolution fusion | flops 7752122368 | bytes 23126016 | tf_op jit(solution)/shard_map/dot_general | solution.py:24
  254.4 0.0 reduce-scatter.5.cloned.1.call-update
  254.4 88.4 %reduce-scatter.5.cloned.1.call-done = f32[64,2048]{1,0:T(8,128)} async-done(((f32[512,2048]{1,0:T(8,128)}), f32[64,2048]{1,0:T(8,128)}) %reduce-scatter.5.cloned.1.call-update) | async-done | bytes 524304 | tf_op jit(solution)/shard_map/reduce_scatter | solution.py:23
  342.8 1.8 convert_element_type.7
Async XLA Ops:
  6.5 54.8 %all-gather.3.cloned.1.call-start = ((), (), s32[]{:S(2)}) async-start(), calls=%async_computation.2 | async-start | bytes 2359296 | tf_op jit(solution)/shard_map/all_gather | solution.py:9
  7.3 195.5 %reduce-scatter.3.cloned.1.call-start = ((), (), s32[]{:S(2)}) async-start(), calls=%async_computation.3 | async-start | bytes 18923520 | tf_op jit(solution)/shard_map/reduce_scatter | solution.py:13
  91.2 0.9 copy-start
  91.2 149.1 %copy-start.1 = (f32[2048]{0:T(1024)S(1)}, f32[2048]{0:T(1024)}, u32[]{:S(2)}) copy-start(f32[2048]{0:T(1024)} %param.11) | copy-start | bytes 24580
  91.2 149.1 %all-gather.5.cloned.1.call-start = ((), (), s32[]{:S(2)}) async-start(), calls=%async_computation.4 | async-start | bytes 4730880 | tf_op jit(solution)/shard_map/all_gather | solution.py:22
  207.5 135.3 %reduce-scatter.5.cloned.1.call-start = ((), (), s32[]{:S(2)}) async-start(), calls=%async_computation.5 | async-start | bytes 4718592 | tf_op jit(solution)/shard_map/reduce_scatter | solution.py:23
Sparse Core Ops, SparseCore 0:
  9.5 51.7 all-gather.2
  91.3 111.3 reduce-scatter.2
  207.7 32.6 all-gather.4
  254.5 88.2 reduce-scatter.4
where the time goes:
time: 351 us
  waiting for transfers between devices  287 us (82%)
  matrix products  37.7 us (11%)
  between operations  13.2 us (4%)
  other arithmetic  12.8 us (4%)
    reduce_scatter x1, waiting for transfers between devices, body(): lax.psum_scatter(jnp.concatenate([gate_part, up_part], axis=1), 'col', sc...  111 us
    reduce_scatter x1, waiting for transfers between devices, body(): lax.psum_scatter(jnp.dot(hidden, down_quant, preferred_element_type=jnp.f...  88.4 us
    all_gather x1, waiting for transfers between devices, body(): gathered = lax.all_gather(act_quant, 'row', axis=0, tiled=True)  54 us
    all_gather x1, waiting for transfers between devices, body(): hidden = lax.all_gather(hidden, 'col', axis=0, tiled=True)  32.7 us
    dot_general x1, matrix products, body(): jnp.dot(hidden, down_quant, preferred_element_type=jnp.float32)  14.1 us
    dot_general x1, matrix products, body(): jnp.dot(gathered, gate_up_quant[0], preferred_element_type=jnp.float32)  11.8 us
    dot_general x1, matrix products, body(): jnp.dot(gathered, gate_up_quant[1], preferred_element_type=jnp.float32)  11.8 us
  transfers between devices with their start and end apart: 4, of which 4 were waited for; matrix products, arithmetic and copies ran while one was open for 0% of the time, Pallas kernels for 0%

commit v1 on v0

v1 whole, which is shorter than its diff:
```python
import functools

import jax
import jax.numpy as jnp
from jax import lax
from jax.experimental import pallas as pl
from jax.experimental.pallas import tpu as pltpu
from jax.sharding import PartitionSpec as P

MESH = pl.DeviceIdType.MESH
SUB = 16
TILE = 512
F32, BF16 = jnp.float32, jnp.bfloat16


def for_tiles(width, fn):
    full = width // TILE
    if full:
        def step(j, carry):
            fn(pl.multiple_of(j * TILE, TILE), TILE)
            return carry
        lax.fori_loop(0, full, step, 0)
    if width % TILE:
        fn(full * TILE, width % TILE)


def kernel(K, Rz, Ry, X, act, act_scale, gu_hbm, gu_scale, down_hbm, down_scale, out,
           wgu, wdn, acts, keep, dsend, drecv, xsend, xrecv, hid, opart, ysend, yrecv, zsend, zrecv, zown,
           w_sem, az_s, az_r, ay_s, ay_r, d_s, d_r, x_s, x_r, h_s, h_r, f_s, f_r, y_s, y_r, z_s, z_r, credit):
    R, C = Rz * Ry, X * 2
    Fl, Dl = wgu.shape[1], wgu.shape[2]
    half = R * SUB // 2
    own = R * SUB // C
    nb = R // C
    row, col = lax.axis_index("row"), lax.axis_index("col")
    z, y = row // Ry, lax.rem(row, Ry)
    x, core = col // 2, lax.rem(col, 2)
    pos = core * X + x
    partner = {"row": row, "col": x * 2 + 1 - core}

    def zdev(dz):
        return {"row": lax.rem(z + dz, Rz) * Ry + y, "col": col}

    def ydev(dy):
        return {"row": z * Ry + lax.rem(y + dy, Ry), "col": col}

    def xdev(dx):
        return {"row": row, "col": lax.rem(x + dx, X) * 2 + core}

    def remote(src, dst, s, r, dev):
        return pltpu.make_async_remote_copy(src_ref=src, dst_ref=dst, send_sem=s, recv_sem=r,
                                            device_id=dev, device_id_type=MESH)

    wcopies = []
    cut = Fl // 2 // SUB * SUB
    for g in range(2):
        for h, part in enumerate((pl.ds(0, cut), pl.ds(cut, Fl - cut))):
            wcopies.append(pltpu.make_async_copy(gu_hbm.at[g, part], wgu.at[g, part], w_sem.at[g * 2 + h]))
    dcopy = pltpu.make_async_copy(down_hbm, wdn, w_sem.at[4])
    for c in wcopies:
        c.start()
    dcopy.start()

    barrier = pltpu.get_barrier_semaphore()
    peers = ([zdev(d) for d in range(1, Rz)] + [ydev(d) for d in range(1, Ry)]
             + [xdev(d) for d in range(1, X)] + [partner])
    for p in peers:
        pl.semaphore_signal(barrier, inc=1, device_id=p, device_id_type=MESH)
    pl.semaphore_wait(barrier, len(peers))

    az = [[remote(act.at[pl.ds(k * SUB, SUB)], acts.at[k, z, y], az_s.at[k, d - 1], az_r.at[k, d - 1], zdev(d))
           for d in range(1, Rz)] for k in range(K)]
    ay = [[remote(acts.at[k, :, y], acts.at[k, :, y], ay_s.at[k, d - 1], ay_r.at[k, d - 1], ydev(d))
           for d in range(1, Ry)] for k in range(K)]
    for k in range(K):
        for c in az[k]:
            c.start()
    for k in range(K):
        acts[k, z, y] = act[k * SUB:(k + 1) * SUB, :]

    def forward_acts(k):
        for c in az[k]:
            c.wait_recv()
        for c in ay[k]:
            c.start()

    dd = [remote(dsend, drecv, d_s.at[k], d_r.at[k], partner) for k in range(K)]
    xx = [[remote(xsend.at[k % 2, d - 1], xrecv.at[k, d - 1], x_s.at[k, d - 1], x_r.at[k, d - 1], xdev(d))
           for d in range(1, X)] for k in range(K)]
    hh = [[remote(hid.at[k, pos], hid.at[k, pos], h_s.at[k, d - 1], h_r.at[k, d - 1], xdev(d))
           for d in range(1, X)] for k in range(K)]
    ff = [remote(hid.at[k, pl.ds(core * X, X)], hid.at[k, pl.ds(core * X, X)], f_s.at[k], f_r.at[k], partner)
          for k in range(K)]
    yy = [[remote(ysend.at[k % 2, d - 1], yrecv.at[k, d - 1], y_s.at[k, d - 1], y_r.at[k, d - 1], ydev(d))
           for d in range(1, Ry)] for k in range(K)]
    zz = [[remote(zsend.at[k % 2, d - 1], zrecv.at[k, d - 1], z_s.at[k, d - 1], z_r.at[k, d - 1], zdev(d))
           for d in range(1, Rz)] for k in range(K)]

    def stage_g(k):
        for c in ay[k]:
            c.wait_recv()
        if k + 1 < K:
            forward_acts(k + 1)
        if k == 0:
            for c in wcopies:
                c.wait()
        else:
            dd[k - 1].wait_send()
        blocks = Rz // 2
        for g in range(2):
            def tile(start, size, g=g):
                lhs = jnp.concatenate([
                    acts[k, pl.ds(core * blocks, blocks)].reshape(half, Dl),
                    acts[k, pl.ds((1 - core) * blocks, blocks)].reshape(half, Dl)], axis=0)
                r = lax.dot_general(lhs, wgu[g, pl.ds(start, size), :], (((1,), (1,)), ((), ())),
                                    preferred_element_type=F32)
                keep[k % 2, g, :, pl.ds(start, size)] = r[:half]
                dsend[g, :, pl.ds(start, size)] = r[half:]
            for_tiles(Fl, tile)
        if k >= 1:
            pl.semaphore_wait(credit, 1)
        dd[k].start()

    def stage_x(k):
        dd[k].wait_recv()
        if k >= 2:
            for c in xx[k - 2]:
                c.wait_send()
        for d in range(1, X):
            rows = pl.ds(pl.multiple_of(lax.rem(x + d, X) * own, own), own)
            for g in range(2):
                def tile(start, size, g=g, rows=rows, d=d):
                    cols = pl.ds(start, size)
                    xsend[k % 2, d - 1, g, :, cols] = (keep[k % 2, g, rows, cols] + drecv[g, rows, cols]).astype(BF16)
                for_tiles(Fl, tile)
            xx[k][d - 1].start()
        rows = pl.ds(pl.multiple_of(x * own, own), own)
        for g in range(2):
            def tile(start, size, g=g):
                cols = pl.ds(start, size)
                keep[k % 2, g, rows, cols] = keep[k % 2, g, rows, cols] + drecv[g, rows, cols]
            for_tiles(Fl, tile)
        if k + 1 < K:
            pl.semaphore_signal(credit, inc=1, device_id=partner, device_id_type=MESH)

    def stage_s(k):
        for c in xx[k]:
            c.wait_recv()
        rows = pl.ds(pl.multiple_of(x * own, own), own)
        scale = jnp.concatenate([act_scale[pos * nb + i, k] for i in range(nb)], axis=0)

        def tile(start, size):
            cols = pl.ds(start, size)
            vals = []
            for g in range(2):
                v = keep[k % 2, g, rows, cols]
                for d in range(1, X):
                    v = v + xrecv[k, d - 1, g, :, cols].astype(F32)
                vals.append(v * scale * gu_scale[g:g + 1, cols])
            hid[k, pos, :, cols] = (vals[0] / (1.0 + jnp.exp(-vals[0])) * vals[1]).astype(BF16)
        for_tiles(Fl, tile)
        for c in hh[k]:
            c.start()

    def stage_d(k):
        for c in hh[k]:
            c.wait_recv()
        ff[k].start()
        if k == 0:
            dcopy.wait()
        if k >= 2:
            for c in yy[k - 2]:
                c.wait_send()
        ff[k].wait_recv()

        def tile(start, size):
            r = jnp.dot(hid[k].reshape(R * SUB, Fl), wdn[:, pl.ds(start, size)], preferred_element_type=F32)
            opart[:, :, :, pl.ds(start, size)] = r.reshape(Rz, Ry, SUB, size)
        for_tiles(Dl, tile)
        for d in range(1, Ry):
            ysend[k % 2, d - 1] = opart[:, lax.rem(y + d, Ry)].astype(BF16)
            yy[k][d - 1].start()

    def stage_y(k):
        for c in yy[k]:
            c.wait_recv()
        if k >= 2:
            for c in zz[k - 2]:
                c.wait_send()
        for d in range(1, Rz + 1):
            zt = lax.rem(z + d, Rz)
            v = opart[zt, y]
            for e in range(1, Ry):
                v = v + yrecv[k, e - 1, zt].astype(F32)
            if d < Rz:
                zsend[k % 2, d - 1] = v.astype(BF16)
                zz[k][d - 1].start()
            else:
                zown[k] = v

    def stage_z(k):
        for c in zz[k]:
            c.wait_recv()
        v = zown[k]
        for d in range(1, Rz):
            v = v + zrecv[k, d - 1].astype(F32)
        out[k * SUB:(k + 1) * SUB, :] = (v * down_scale[...]).astype(BF16)

    forward_acts(0)
    for it in range(K + 3):
        if it < K:
            stage_g(it)
            stage_x(it)
        if 0 <= it - 1 < K:
            stage_s(it - 1)
        if 0 <= it - 3 < K:
            stage_y(it - 3)
        if 0 <= it - 2 < K:
            stage_d(it - 2)
    for k in range(K):
        stage_z(k)

    for k in range(K):
        for c in az[k] + ay[k] + hh[k] + [ff[k]]:
            c.wait_send()
    dd[K - 1].wait_send()
    for k in range(max(K - 2, 0), K):
        for c in xx[k] + yy[k] + zz[k]:
            c.wait_send()


def solution(mesh):
    R, C = mesh.shape["row"], mesh.shape["col"]
    X = C // 2
    Ry = max(d for d in range(1, R + 1) if R % d == 0 and d * d <= R)
    Rz = R // Ry

    def body(act, act_scale, gu, gu_scale, down, down_scale):
        tpr, Dl = act.shape
        Fl = gu.shape[2]
        K = tpr // SUB
        T = R * SUB
        own = T // C
        vmem = pl.BlockSpec(memory_space=pltpu.VMEM)
        hbm = pl.BlockSpec(memory_space=pl.ANY)
        dma = pltpu.SemaphoreType.DMA
        scratch = [
            pltpu.VMEM((2, Fl, Dl), BF16),
            pltpu.VMEM((Fl, Dl), BF16),
            pltpu.VMEM((K, Rz, Ry, SUB, Dl), BF16),
            pltpu.VMEM((2, 2, T // 2, Fl), F32),
            pltpu.VMEM((2, T // 2, Fl), F32),
            pltpu.VMEM((2, T // 2, Fl), F32),
            pltpu.VMEM((2, X - 1, 2, own, Fl), BF16),
            pltpu.VMEM((K, X - 1, 2, own, Fl), BF16),
            pltpu.VMEM((K, C, own, Fl), BF16),
            pltpu.VMEM((Rz, Ry, SUB, Dl), F32),
            pltpu.VMEM((2, Ry - 1, Rz, SUB, Dl), BF16),
            pltpu.VMEM((K, Ry - 1, Rz, SUB, Dl), BF16),
            pltpu.VMEM((2, Rz - 1, SUB, Dl), BF16),
            pltpu.VMEM((K, Rz - 1, SUB, Dl), BF16),
            pltpu.VMEM((K, SUB, Dl), F32),
            dma((5,)),
            dma((K, Rz - 1)), dma((K, Rz - 1)),
            dma((K, Ry - 1)), dma((K, Ry - 1)),
            dma((K,)), dma((K,)),
            dma((K, X - 1)), dma((K, X - 1)),
            dma((K, X - 1)), dma((K, X - 1)),
            dma((K,)), dma((K,)),
            dma((K, Ry - 1)), dma((K, Ry - 1)),
            dma((K, Rz - 1)), dma((K, Rz - 1)),
            pltpu.SemaphoreType.REGULAR,
        ]
        return pl.pallas_call(
            functools.partial(kernel, K, Rz, Ry, X),
            out_shape=jax.ShapeDtypeStruct((tpr, Dl), BF16),
            in_specs=[vmem, vmem, hbm, vmem, hbm, vmem],
            out_specs=vmem,
            scratch_shapes=scratch,
            compiler_params=pltpu.CompilerParams(
                collective_id=0, has_side_effects=True, vmem_limit_bytes=67043328
            ),
        )(act, act_scale.reshape(R, K, SUB, 1), jnp.swapaxes(gu, 1, 2), gu_scale, down, down_scale.reshape(1, Dl))

    in_specs = (P("row", "col"), P(), P(None, "col", "row"), P(None, "row"), P("row", "col"), P("col"))
    return jax.shard_map(body, mesh=mesh, in_specs=in_specs, out_specs=P("row", "col"), check_vma=False)
```

time: 351 us -> 148 us (0.42)
  waiting for transfers between devices: 287 us -> 0 us
  Pallas kernels: 0 us -> 145 us
  matrix products: 37.7 us -> 0 us
  between operations: 13.2 us -> 0.01 us
  other arithmetic: 12.8 us -> 0 us
    reduce_scatter x2 -> x0, waiting for transfers between devices: 199 us -> none  [the longest x1 111 us: body(): lax.psum_scatter(jnp.concatenate([gate_part, up_part], axis=1), 'col', sc...]
    pallas_call x0 -> x1, Pallas kernels: none -> 145 us  [body(): pl.pallas_call(functools.partial(kernel, K, Rz, Ry, X), out_shape=jax.Sha...]
    all_gather x2 -> x0, waiting for transfers between devices: 86.7 us -> none  [the longest x1 54 us: body(): gathered = lax.all_gather(act_quant, 'row', axis=0, tiled=True)]
    dot_general x3 -> x0, matrix products: 37.7 us -> none  [the longest x1 14.1 us: body(): jnp.dot(hidden, down_quant, preferred_element_type=jnp.float32)]
    convert_element_type x2 -> x0, other arithmetic: 6.58 us -> none  [the longest x1 4.8 us: body(): hidden = (jax.nn.silu(gate_val) * up_val).astype(jnp.bfloat16)]
    concatenate x1 -> x0, other arithmetic: 6.24 us -> none  [body(): jnp.concatenate([gate_part, up_part], axis=1)]
  transfers between devices with their start and end apart: 4 -> 0, of which waited for: 4 -> 0; matrix products, arithmetic and copies ran while one was open for 0% -> 0% of each run, Pallas kernels for 0% -> 0%
where the time goes in v1:
time: 148 us
  Pallas kernels  145 us (98%)
  local copies, waits for them, and re-layouts  3.26 us (2%)
    pallas_call x1, Pallas kernels, body(): pl.pallas_call(functools.partial(kernel, K, Rz, Ry, X), out_shape=jax.Sha...  145 us

profile of v1, /device:TPU:0, one launch (start us, length us, event | category | flops | bytes accessed | tf_op | source)
XLA Modules:
  0.0 148.1 jit_solution(11304451416241248872)
XLA Ops:
  0.0 1.6 %reshape.8.act_scale = f32[8,4,16,1]{3,2,1,0:T(8,128)} reshape(f32[512]{0:T(512)} %param.7) | data formatting | bytes 4096 | tf_op jit(solution)/shard_map/reshape | solution.py:283
  1.6 144.8 %shard_map.64 = bf16[64,2048]{1,0:T(8,128)(2,1)} custom-call(bf16[64,2048]{1,0:T(8,128)(2,1)} %act.1, f32[8,4,16,1]{3,2,1,0:T(8,128)} %reshape.8.act_scale, bf16[2,3696,2048]{2,1,0:T(8,128)(2,1)} %bitcast.2, f32[2,3696]{1,0:T(2,128)} %gu_scale.1, bf16[3696,2048]{1,0:T(8,128)(2,1)} %down_hbm.1, f32[1,2048]{1,0:T(1,128)} %bitcast.3), custom_call_target="tpu_custom_call" | custom-call | tf_op jit(solution)/shard_map/pallas_call | solution.py:274
  146.4 1.7 %copy.9 = bf16[64,2048]{1,0:T(8,128)(2,1)} copy(bf16[64,2048]{1,0:T(8,128)(2,1)} %shard_map.64) | data formatting | bytes 524288
